TPU v7x, 32 devices: a whole 2x2x4 slice. The times are simulated.
32 devices in a mesh: dp: 2 (over y), expert: 8 (over z, x), etp: 2 (over core).
Axes of the slice: x: 2, y: 2, z: 4, core: 2. Of those that a mesh axis runs over, the one named last changes fastest.
Arguments:
- tokens: bfloat16 [1024, 4096], P(('dp', 'expert'), 'etp'), may hold values from -6 to 6
- expert_ids: int32 [1024, 8], P(('dp', 'expert')), may hold values from 0 to 15, all different within a row; in each aligned block of 64 rows (0 to 63, 64 to 127, ...) at most 48 rows name the same one
- combine: float32 [1024, 8], P(('dp', 'expert')), may hold values from 0.05 to 1
- gate_weight: bfloat16 [16, 4096, 1536], P('expert', 'dp', 'etp'), may hold values from -0.09375 to 0.09375
- up_weight: bfloat16 [16, 4096, 1536], P('expert', 'dp', 'etp'), may hold values from -0.09375 to 0.09375
- down_weight: bfloat16 [16, 1536, 4096], P('expert', 'etp', 'dp'), may hold values from -0.15625 to 0.15625
Outputs:
- mixed: bfloat16 [1024, 4096], P(('dp', 'expert'), 'etp')
Inputs may be any that keep to these rules, and one draw needn't show every extreme that they name: `expert_ids`: each row names 8 different experts. In the rows of one device (aligned blocks of 64 rows) no expert is named by more than 48 rows, a bound that some block reaches.
All inputs are finite; a program needn't handle non-finite values.
Results may differ from a plain program's by a relative error of at most 0.008.
Values may be sent and summed in bfloat16 or wider, within the bound.
A program may use at most 192 MiB of HBM per device.

v0:
```python
import jax
import jax.numpy as jnp
from jax import lax
from jax.sharding import PartitionSpec as P


def shards(tokens, expert_ids, combine, gate_weight, up_weight, down_weight):
    tok_rows, top_count = expert_ids.shape
    held_count = gate_weight.shape[0]
    groups = lax.axis_size("expert")
    experts = held_count * groups
    capacity = min(tok_rows, 3 * tok_rows * top_count // (2 * experts))
    slots_all = experts * capacity
    onehot = (expert_ids[:, :, None] == jnp.arange(experts, dtype=jnp.int32)[None, None, :]).astype(
        jnp.int32
    )
    flattened = onehot.reshape(tok_rows * top_count, experts)
    before = jnp.cumsum(flattened, axis=0) - flattened
    slot_index = jnp.sum(before * flattened, axis=1).reshape(tok_rows, top_count)
    target = expert_ids * capacity + slot_index
    matches = target[:, :, None] == jnp.arange(slots_all, dtype=jnp.int32)[None, None, :]
    picker = jnp.any(matches, axis=1).astype(jnp.bfloat16)
    weights_map = jnp.sum(jnp.where(matches, combine[:, :, None], 0.0), axis=1)
    gathered = lax.all_gather(tokens, "etp", axis=1, tiled=True)
    packed = jnp.einsum("ts,td->sd", picker, gathered, preferred_element_type=jnp.float32).astype(
        jnp.bfloat16
    )
    arrived = lax.all_to_all(
        packed.reshape(groups, held_count, capacity, gathered.shape[1]),
        "expert",
        split_axis=0,
        concat_axis=2,
        tiled=True,
    )
    inputs = arrived[0]
    gate_part = jnp.einsum(
        "erd,edf->erf",
        inputs,
        lax.all_gather(gate_weight, "dp", axis=1, tiled=True),
        preferred_element_type=jnp.float32,
    )
    up_part = jnp.einsum(
        "erd,edf->erf",
        inputs,
        lax.all_gather(up_weight, "dp", axis=1, tiled=True),
        preferred_element_type=jnp.float32,
    )
    hidden = (jax.nn.silu(gate_part) * up_part).astype(jnp.bfloat16)
    partial_value = jnp.einsum(
        "erf,efd->erd",
        hidden,
        lax.all_gather(down_weight, "dp", axis=2, tiled=True),
        preferred_element_type=jnp.float32,
    ).astype(jnp.bfloat16)
    partial_value = lax.optimization_barrier(partial_value)
    summed = lax.psum_scatter(
        partial_value.astype(jnp.float32).astype(jnp.bfloat16),
        "etp",
        scatter_dimension=2,
        tiled=True,
    )
    returned_rows = lax.all_to_all(summed[None], "expert", split_axis=2, concat_axis=0, tiled=True)
    returned_rows = returned_rows.reshape(slots_all, returned_rows.shape[3])
    weight_high = weights_map.astype(jnp.bfloat16)
    weight_low = (weights_map - weight_high.astype(jnp.float32)).astype(jnp.bfloat16)
    result = jnp.dot(weight_high, returned_rows, preferred_element_type=jnp.float32)
    result = result + jnp.dot(weight_low, returned_rows, preferred_element_type=jnp.float32)
    return result.astype(jnp.bfloat16)


def solution(mesh):
    placed = (
        P(("dp", "expert"), "etp"),
        P(("dp", "expert"), None),
        P(("dp", "expert"), None),
        P("expert", "dp", "etp"),
        P("expert", "dp", "etp"),
        P("expert", "etp", "dp"),
    )
    return jax.shard_map(
        shards, mesh=mesh, in_specs=placed, out_specs=P(("dp", "expert"), "etp"), check_vma=False
    )
```

profile of v0, /device:TPU:0, one launch (start us, length us, event | category | flops | bytes accessed | tf_op | source)
XLA Modules:
  0.0 599.1 jit_solution(10712536201870545837)
XLA Ops:
  6.5 0.0 all-gather.4.cloned.1.call-start
  6.5 0.7 all-gather.4.cloned.1.call-update
  7.3 0.0 copy-start.1
  7.3 0.0 copy-start
  7.3 0.0 all-gather.6.cloned.1.call-start
  7.3 0.7 all-gather.6.cloned.1.call-update
  8.0 0.0 copy-done.1
  8.0 0.1 copy.46
  8.1 0.1 eq.43
  8.2 0.1 eq.39
  8.3 1.2 reduce-window.6
  9.5 0.2 slice_reduce_fusion
  9.7 0.1 fusion.7
  9.8 0.1 reshape.32
  9.9 0.1 copy.49
  10.0 0.1 copy.50
  10.1 0.0 copy-done
  10.1 2.3 all_gather.12
  12.4 0.5 fusion.1
  12.9 4.5 convolution_convert_fusion.1
  17.4 7.8 %all-to-all-start = ((bf16[8,2,48,4096]{3,2,1,0:T(8,128)(2,1)}), bf16[8,2,48,4096]{3,2,1,0:T(8,128)(2,1)}, u32[]{:S(2)}, u32[]{:S(2)}) async-start(bf16[8,2,48,4096]{3,2,1,0:T(8,128)(2,1)} %bitcast.38), calls=%async_computation | async-start | bytes 12582912 | tf_op jit(solution)/shard_map/all_to_all | solution.py:28
  25.3 0.0 all-gather.8.cloned.1.call-start
  25.3 0.7 all-gather.8.cloned.1.call-update
  26.0 0.2 reduce-scatter.2.cloned.1.call-start
  26.2 137.6 %all-to-all-done = bf16[8,2,48,4096]{3,2,1,0:T(8,128)(2,1)} async-done(((bf16[8,2,48,4096]{3,2,1,0:T(8,128)(2,1)}), bf16[8,2,48,4096]{3,2,1,0:T(8,128)(2,1)}, u32[]{:S(2)}, u32[]{:S(2)}) %all-to-all-start) | async-done | bytes 6291488 | tf_op jit(solution)/shard_map/all_to_all | solution.py:28
  163.8 6.2 %copy.52 = bf16[1,2,8,48,4096]{4,3,2,1,0:T(8,128)(2,1)} copy(bf16[1,2,8,48,4096]{4,3,1,2,0:T(8,128)(2,1)} %bitcast.3) | data formatting | bytes 12582912 | tf_op jit(solution)/shard_map/all_to_all | solution.py:28
  170.0 0.0 all-gather.4.cloned.1.call-done
  170.0 12.9 %fusion.10 = f32[2,384,768]{2,1,0:T(8,128)S(1)} fusion(bf16[2,384,4096]{2,1,0:T(8,128)(2,1)} %bitcast.42, bf16[2,4096,768]{2,1,0:T(8,128)(2,1)} %all-gather.4.cloned.1.call-done), kind=kOutput, calls=%fused_computation.23 | convolution fusion | flops 4831838208 | bytes 21233664 | tf_op jit(solution)/shard_map/erd,edf->erf/dot_general | solution.py:36
  182.9 133.3 %all-gather.6.cloned.1.call-done = bf16[2,4096,768]{2,1,0:T(8,128)(2,1)} async-done(((bf16[2,2048,768]{2,1,0:T(8,128)(2,1)}), bf16[2,4096,768]{2,1,0:T(8,128)(2,1)}) %all-gather.6.cloned.1.call-update) | async-done | bytes 12582928 | tf_op jit(solution)/shard_map/all_gather | solution.py:45
  316.2 154.1 %all-gather.8.cloned.1.call-done = bf16[2,768,4096]{2,1,0:T(8,128)(2,1)} async-done(((bf16[2,768,2048]{2,1,0:T(8,128)(2,1)}), bf16[2,768,4096]{2,1,0:T(8,128)(2,1)}) %all-gather.8.cloned.1.call-update) | async-done | bytes 12582928 | tf_op jit(solution)/shard_map/all_gather | solution.py:52
  470.3 20.5 %convolution_convert_fusion = bf16[2,384,4096]{2,1,0:T(8,128)(2,1)} fusion(bf16[2,768,4096]{2,1,0:T(8,128)(2,1)} %all-gather.8.cloned.1.call-done, f32[2,384,768]{2,1,0:T(8,128)S(1)} %fusion.10, bf16[2,384,4096]{2,1,0:T(8,128)(2,1)} %bitcast.43, bf16[2,4096,768]{2,1,0:T(8,128)(2,1)} %all-gather.6.cloned.1.call-done), kind=kOutput, calls=%fused_computation | convolution fusion | flops 9670361088 | bytes 40108032 | tf_op jit(solution)/shard_map/erf,efd->erd/dot_general | solution.py:49
  490.9 0.0 reduce-scatter.2.cloned.1.call-update
  490.9 14.0 %reduce-scatter.2.cloned.1.call-done = bf16[2,384,2048]{2,1,0:T(8,128)(2,1)} async-done(((bf16[2,384,4096]{2,1,0:T(8,128)(2,1)}), bf16[2,384,2048]{2,1,0:T(8,128)(2,1)}) %reduce-scatter.2.cloned.1.call-update) | async-done | bytes 3145744 | tf_op jit(solution)/shard_map/reduce_scatter | solution.py:56
  504.9 6.8 %copy.53 = bf16[1,2,384,2048]{3,1,0,2:T(2,128)(2,1)} copy(bf16[1,2,384,2048]{3,2,1,0:T(8,128)(2,1)} %bitcast.44) | data formatting | bytes 6291456 | tf_op jit(solution)/shard_map/broadcast_in_dim | solution.py:62
  511.7 0.0 copy-start.2
  511.7 6.0 %all-to-all-start.1 = ((bf16[1,2,384,2048]{3,1,0,2:T(2,128)(2,1)}), bf16[1,2,384,2048]{3,1,0,2:T(2,128)(2,1)S(1)}, u32[]{:S(2)}, u32[]{:S(2)}) async-start(bf16[1,2,384,2048]{3,1,0,2:T(2,128)(2,1)} %copy.53), calls=%async_computation.2 | async-start | bytes 6291456 | tf_op jit(solution)/shard_map/all_to_all | solution.py:62
  517.8 0.0 copy-done.2
  517.8 0.1 copy.51
  517.8 0.5 select_reduce_fusion
  518.4 70.4 %all-to-all-done.1 = bf16[1,2,384,2048]{3,1,0,2:T(2,128)(2,1)S(1)} async-done(((bf16[1,2,384,2048]{3,1,0,2:T(2,128)(2,1)}), bf16[1,2,384,2048]{3,1,0,2:T(2,128)(2,1)S(1)}, u32[]{:S(2)}, u32[]{:S(2)}) %all-to-all-start.1) | async-done | bytes 3145760 | tf_op jit(solution)/shard_map/all_to_all | solution.py:62
  588.8 1.4 copy.54
  590.1 0.4 copy.55
  590.6 0.7 fusion.3
  591.2 1.4 fusion
  (4 shorter events, 0.1 us)
Async XLA Ops:
  6.5 163.5 %all-gather.4.cloned.1.call-start = ((), (), s32[]{:S(2)}) async-start(), calls=%async_computation.3 | async-start | bytes 18874368 | tf_op jit(solution)/shard_map/all_gather | solution.py:39
  7.3 0.8 copy-start.1
  7.3 2.8 copy-start
  7.3 309.0 %all-gather.6.cloned.1.call-start = ((), (), s32[]{:S(2)}) async-start(), calls=%async_computation.4 | async-start | bytes 18874368 | tf_op jit(solution)/shard_map/all_gather | solution.py:45
  17.4 146.3 %all-to-all-start = ((bf16[8,2,48,4096]{3,2,1,0:T(8,128)(2,1)}), bf16[8,2,48,4096]{3,2,1,0:T(8,128)(2,1)}, u32[]{:S(2)}, u32[]{:S(2)}) async-start(bf16[8,2,48,4096]{3,2,1,0:T(8,128)(2,1)} %bitcast.38), calls=%async_computation | async-start | bytes 12582912 | tf_op jit(solution)/shard_map/all_to_all | solution.py:28
  25.3 445.1 %all-gather.8.cloned.1.call-start = ((), (), s32[]{:S(2)}) async-start(), calls=%async_computation.5 | async-start | bytes 18874368 | tf_op jit(solution)/shard_map/all_gather | solution.py:52
  26.0 478.9 %reduce-scatter.2.cloned.1.call-start = ((), (), s32[]{:S(2)}) async-start(), calls=%async_computation.6 | async-start | bytes 9437184 | tf_op jit(solution)/shard_map/reduce_scatter | solution.py:56
  511.7 6.0 %copy-start.2 = (f32[64,8]{0,1:T(8,128)S(1)}, f32[64,8]{0,1:T(8,128)}, u32[]{:S(2)}) copy-start(f32[64,8]{0,1:T(8,128)} %param.8) | copy-start | bytes 6148
  511.7 77.1 %all-to-all-start.1 = ((bf16[1,2,384,2048]{3,1,0,2:T(2,128)(2,1)}), bf16[1,2,384,2048]{3,1,0,2:T(2,128)(2,1)S(1)}, u32[]{:S(2)}, u32[]{:S(2)}) async-start(bf16[1,2,384,2048]{3,1,0,2:T(2,128)(2,1)} %copy.53), calls=%async_computation.2 | async-start | bytes 6291456 | tf_op jit(solution)/shard_map/all_to_all | solution.py:62
Sparse Core Ops, SparseCore 0:
  8.9 154.2 all-gather.3
  164.7 151.4 all-gather.5
  317.8 152.4 all-gather.7
  491.0 13.8 reduce-scatter.1
where the time goes:
time: 600 us; the launch traced here: 599 us
  waiting for transfers between devices  511 us (85%)
  matrix products  40 us (7%)
  local copies, waits for them, and re-layouts  15.7 us (3%)
  starting transfers between devices  14.2 us (2%)
  between operations  13.2 us (2%)
    all_gather x1, waiting for transfers between devices, shards(): lax.all_gather(down_weight, 'dp', axis=2, tiled=True)  154 us
    all_to_all x1, waiting for transfers between devices, shards(): lax.all_to_all(packed.reshape(groups, held_count, capacity, gathered.shap...  138 us
    all_gather x1, waiting for transfers between devices, shards(): lax.all_gather(up_weight, 'dp', axis=1, tiled=True)  133 us
    all_to_all x1, waiting for transfers between devices, shards(): lax.all_to_all(summed[None], 'expert', split_axis=2, concat_axis=0, tiled...  70.4 us
    dot_general x1, matrix products, shards(): jnp.einsum('erf,efd->erd', hidden, lax.all_gather(down_weight, 'dp', axis...  20.5 us
    reduce_scatter x1, waiting for transfers between devices, shards(): lax.psum_scatter(partial_value.astype(jnp.float32).astype(jnp.bfloat16),...  14 us
    dot_general x1, matrix products, shards(): jnp.einsum('erd,edf->erf', inputs, lax.all_gather(gate_weight, 'dp', axis...  12.9 us
  transfers between devices with their start and end apart: 6, of which 5 were waited for; matrix products, arithmetic and copies ran while one was open for 4% of the time, Pallas kernels for 0%

commit v1 on v0

--- a/solution.py
+++ b/solution.py
@@ -39,12 +39,24 @@
         lax.all_gather(gate_weight, "dp", axis=1, tiled=True),
         preferred_element_type=jnp.float32,
     )
+    big, m_next = (lax.axis_size("dp"), lax.axis_index("dp"))
+    line_up = [(idx, (idx - 1) % big) for idx in range(big)]
+    view_out = up_weight.shape[1]
+    z = up_weight
     up_part = jnp.einsum(
         "erd,edf->erf",
-        inputs,
-        lax.all_gather(up_weight, "dp", axis=1, tiled=True),
+        lax.dynamic_slice_in_dim(inputs, m_next * view_out, z.shape[1], axis=2),
+        z,
         preferred_element_type=jnp.float32,
     )
+    for num in [*range(1, big)]:
+        z = lax.ppermute(z, "dp", line_up)
+        up_part = up_part + jnp.einsum(
+            "erd,edf->erf",
+            lax.dynamic_slice_in_dim(inputs, (m_next + num) % big * view_out, z.shape[1], axis=2),
+            z,
+            preferred_element_type=jnp.float32,
+        )
     hidden = (jax.nn.silu(gate_part) * up_part).astype(jnp.bfloat16)
     partial_value = jnp.einsum(
         "erf,efd->erd",

time: 600 us -> 572 us (0.953)
  waiting for transfers between devices: 511 us -> 482 us
    all_gather x1 -> x0, waiting for transfers between devices: 133 us -> none  [shards(): lax.all_gather(up_weight, 'dp', axis=1, tiled=True)]
    all_gather x1, waiting for transfers between devices: 0.01 us -> 125 us  [shards(): lax.all_gather(gate_weight, 'dp', axis=1, tiled=True)]
    all_gather x1, waiting for transfers between devices: 154 us -> 135 us  [shards(): lax.all_gather(down_weight, 'dp', axis=2, tiled=True)]
    dot_general x0 -> x2, matrix products: none -> 11.1 us  [the longest x1 7.08 us: shards(): jnp.einsum('erd,edf->erf', lax.dynamic_slice_in_dim(inputs, (m_next + num...]
    dot_general x1, matrix products: 20.5 us -> 11.5 us  [shards(): jnp.einsum('erf,efd->erd', hidden, lax.all_gather(down_weight, 'dp', axis...]
  transfers between devices with their start and end apart: 6 -> 6, of which waited for: 5 -> 5; matrix products, arithmetic and copies ran while one was open for 4% -> 6% of each run, Pallas kernels for 0% -> 0%
where the time goes in v1:
time: 572 us; the launch traced here: 571 us
  waiting for transfers between devices  482 us (84%)
  matrix products  40.9 us (7%)
  local copies, waits for them, and re-layouts  15.5 us (3%)
  starting transfers between devices  15.4 us (3%)
  between operations  13.3 us (2%)
    all_to_all x1, waiting for transfers between devices, shards(): lax.all_to_all(packed.reshape(groups, held_count, capacity, gathered.shap...  136 us
    all_gather x1, waiting for transfers between devices, shards(): lax.all_gather(down_weight, 'dp', axis=2, tiled=True)  135 us
    all_gather x1, waiting for transfers between devices, shards(): lax.all_gather(gate_weight, 'dp', axis=1, tiled=True)  125 us
    all_to_all x1, waiting for transfers between devices, shards(): lax.all_to_all(summed[None], 'expert', split_axis=2, concat_axis=0, tiled...  70.4 us
    reduce_scatter x1, waiting for transfers between devices, shards(): lax.psum_scatter(partial_value.astype(jnp.float32).astype(jnp.bfloat16),...  14 us
    dot_general x1, matrix products, shards(): jnp.einsum('erd,edf->erf', inputs, lax.all_gather(gate_weight, 'dp', axis...  11.8 us
    dot_general x1, matrix products, shards(): jnp.einsum('erf,efd->erd', hidden, lax.all_gather(down_weight, 'dp', axis...  11.5 us
  transfers between devices with their start and end apart: 6, of which 5 were waited for; matrix products, arithmetic and copies ran while one was open for 6% of the time, Pallas kernels for 0%

profile of v1, /device:TPU:0, one launch (start us, length us, event | category | flops | bytes accessed | tf_op | source)
XLA Modules:
  0.0 571.4 jit_solution(11469917746390633345)
XLA Ops:
  6.5 0.0 all-gather.3.cloned.1.call-start
  6.5 0.7 all-gather.3.cloned.1.call-update
  7.3 0.0 copy-done.3
  7.3 0.1 copy.46
  7.4 0.1 eq.45
  7.4 0.1 eq.41
  7.6 1.2 reduce-window.6
  8.7 0.2 slice_reduce_fusion
  9.0 0.1 fusion.13
  9.1 0.1 reshape.32
  9.2 0.1 copy.49
  9.2 0.1 copy.50
  9.3 0.0 copy-done.2
  9.3 2.3 all_gather.9
  11.6 0.5 fusion.5
  12.2 4.5 convolution_convert_fusion.1
  16.6 7.3 %all-to-all-start = ((bf16[8,2,48,4096]{3,2,1,0:T(8,128)(2,1)}), bf16[8,2,48,4096]{3,2,1,0:T(8,128)(2,1)}, u32[]{:S(2)}, u32[]{:S(2)}) async-start(bf16[8,2,48,4096]{3,2,1,0:T(8,128)(2,1)} %bitcast.39), calls=%async_computation | async-start | bytes 12582912 | tf_op jit(solution)/shard_map/all_to_all | solution.py:28
  23.9 0.0 all-gather.5.cloned.1.call-start
  24.0 0.0 slice-start
  24.0 0.7 all-gather.5.cloned.1.call-update
  24.7 0.2 reduce-scatter.2.cloned.1.call-start
  24.9 1.6 collective-permute-start
  26.5 135.9 %all-to-all-done = bf16[8,2,48,4096]{3,2,1,0:T(8,128)(2,1)} async-done(((bf16[8,2,48,4096]{3,2,1,0:T(8,128)(2,1)}), bf16[8,2,48,4096]{3,2,1,0:T(8,128)(2,1)}, u32[]{:S(2)}, u32[]{:S(2)}) %all-to-all-start) | async-done | bytes 6291488 | tf_op jit(solution)/shard_map/all_to_all | solution.py:28
  162.4 3.4 copy.52
  165.8 0.0 copy-start
  165.8 2.7 copy-done
  168.5 0.0 slice-done
  168.5 0.0 slice-done.1
  168.5 4.0 fusion.2
  172.6 124.9 %all-gather.3.cloned.1.call-done = bf16[2,4096,768]{2,1,0:T(8,128)(2,1)} async-done(((bf16[2,2048,768]{2,1,0:T(8,128)(2,1)}), bf16[2,4096,768]{2,1,0:T(8,128)(2,1)}) %all-gather.3.cloned.1.call-update) | async-done | bytes 12582928 | tf_op jit(solution)/shard_map/all_gather | solution.py:39
  297.5 11.8 %fusion.17 = f32[2,384,768]{2,1,0:T(8,128)S(1)} fusion(bf16[2,384,4096]{2,1,0:T(8,128)(2,1)} %bitcast.44, bf16[2,4096,768]{2,1,0:T(8,128)(2,1)} %all-gather.3.cloned.1.call-done), kind=kOutput, calls=%fused_computation.28 | convolution fusion | flops 4831838208 | bytes 21233664 | tf_op jit(solution)/shard_map/erd,edf->erf/dot_general | solution.py:36
  309.3 0.0 collective-permute-done
  309.3 0.0 copy-done.1
  309.3 0.0 copy-done.5
  309.4 7.1 %multiply_convert_fusion = bf16[2,384,768]{2,1,0:T(8,128)(2,1)S(1)} fusion(f32[2,384,768]{2,1,0:T(8,128)S(1)} %copy-done.5, f32[2,384,768]{2,1,0:T(8,128)S(1)} %fusion.17, bf16[2,2048,768]{2,1,0:T(8,128)(2,1)} %collective-permute-done, bf16[2,384,4096]{2,1,0:T(8,128)(2,1)S(1)} %bitcast.45, s32[]{:T(128)S(6)} %select_n.20), kind=kOutput, calls=%fused_computation.6 | convolution fusion | flops 2420047872 | bytes 15335428 | tf_op jit(solution)/shard_map/erd,edf->erf/dot_general | solution.py:54
  316.4 135.1 %all-gather.5.cloned.1.call-done = bf16[2,768,4096]{2,1,0:T(8,128)(2,1)} async-done(((bf16[2,768,2048]{2,1,0:T(8,128)(2,1)}), bf16[2,768,4096]{2,1,0:T(8,128)(2,1)}) %all-gather.5.cloned.1.call-update) | async-done | bytes 12582928 | tf_op jit(solution)/shard_map/all_gather | solution.py:64
  451.5 11.5 %convolution_convert_fusion = bf16[2,384,4096]{2,1,0:T(8,128)(2,1)} fusion(bf16[2,384,768]{2,1,0:T(8,128)(2,1)S(1)} %multiply_convert_fusion, bf16[2,768,4096]{2,1,0:T(8,128)(2,1)} %all-gather.5.cloned.1.call-done), kind=kOutput, calls=%fused_computation | convolution fusion | flops 4834983936 | bytes 20054016 | tf_op jit(solution)/shard_map/erf,efd->erd/dot_general | solution.py:61
  463.0 0.0 reduce-scatter.2.cloned.1.call-update
  463.0 14.0 %reduce-scatter.2.cloned.1.call-done = bf16[2,384,2048]{2,1,0:T(8,128)(2,1)} async-done(((bf16[2,384,4096]{2,1,0:T(8,128)(2,1)}), bf16[2,384,2048]{2,1,0:T(8,128)(2,1)}) %reduce-scatter.2.cloned.1.call-update) | async-done | bytes 3145744 | tf_op jit(solution)/shard_map/reduce_scatter | solution.py:68
  477.0 6.8 %copy.53 = bf16[1,2,384,2048]{3,1,0,2:T(2,128)(2,1)} copy(bf16[1,2,384,2048]{3,2,1,0:T(8,128)(2,1)} %bitcast.46) | data formatting | bytes 6291456 | tf_op jit(solution)/shard_map/broadcast_in_dim | solution.py:74
  483.8 6.3 %all-to-all-start.1 = ((bf16[1,2,384,2048]{3,1,0,2:T(2,128)(2,1)}), bf16[1,2,384,2048]{3,1,0,2:T(2,128)(2,1)S(1)}, u32[]{:S(2)}, u32[]{:S(2)}) async-start(bf16[1,2,384,2048]{3,1,0,2:T(2,128)(2,1)} %copy.53), calls=%async_computation.2 | async-start | bytes 6291456 | tf_op jit(solution)/shard_map/all_to_all | solution.py:74
  490.1 0.1 copy.51
  490.2 0.5 select_reduce_fusion
  490.7 70.4 %all-to-all-done.1 = bf16[1,2,384,2048]{3,1,0,2:T(2,128)(2,1)S(1)} async-done(((bf16[1,2,384,2048]{3,1,0,2:T(2,128)(2,1)}), bf16[1,2,384,2048]{3,1,0,2:T(2,128)(2,1)S(1)}, u32[]{:S(2)}, u32[]{:S(2)}) %all-to-all-start.1) | async-done | bytes 3145760 | tf_op jit(solution)/shard_map/all_to_all | solution.py:74
  561.1 1.4 copy.54
  562.5 0.4 copy.55
  562.9 0.7 fusion.9
  563.5 1.4 fusion.4
  (12 shorter events, 0.1 us)
Async XLA Ops:
  6.5 0.7 copy-start.3
  6.5 2.8 copy-start.2
  6.5 290.9 %all-gather.3.cloned.1.call-start = ((), (), s32[]{:S(2)}) async-start(), calls=%async_computation.3 | async-start | bytes 18874368 | tf_op jit(solution)/shard_map/all_gather | solution.py:39
  16.6 145.8 %all-to-all-start = ((bf16[8,2,48,4096]{3,2,1,0:T(8,128)(2,1)}), bf16[8,2,48,4096]{3,2,1,0:T(8,128)(2,1)}, u32[]{:S(2)}, u32[]{:S(2)}) async-start(bf16[8,2,48,4096]{3,2,1,0:T(8,128)(2,1)} %bitcast.39), calls=%async_computation | async-start | bytes 12582912 | tf_op jit(solution)/shard_map/all_to_all | solution.py:28
  23.9 427.6 %all-gather.5.cloned.1.call-start = ((), (), s32[]{:S(2)}) async-start(), calls=%async_computation.4 | async-start | bytes 18874368 | tf_op jit(solution)/shard_map/all_gather | solution.py:64
  24.0 144.5 %slice-start = ((s8[6291456]{0:T(1024)(128)(4,1)}), s8[2097152]{0:T(1024)(128)(4,1)S(1)}, s32[]{:S(2)}) async-start(s8[6291456]{0:T(1024)(128)(4,1)} %bitcast.47), calls=%async_computation.6 | async-start | bytes 4194304
  24.7 452.4 %reduce-scatter.2.cloned.1.call-start = ((), (), s32[]{:S(2)}) async-start(), calls=%async_computation.5 | async-start | bytes 9437184 | tf_op jit(solution)/shard_map/reduce_scatter | solution.py:68
  24.9 284.4 %collective-permute-start = (bf16[2,2048,768]{2,1,0:T(8,128)(2,1)}, bf16[2,2048,768]{2,1,0:T(8,128)(2,1)}, u32[]{:S(2)}, u32[]{:S(2)}) collective-permute-start(bf16[2,2048,768]{2,1,0:T(8,128)(2,1)} %param.10), channel_id=1, source_target_pairs={{0,16},{16,0},{1,17},{17,1},{2,18},{18,2},{3,19},{19,3},{4,20},{20... | collective-permute-start | bytes 18874376 | tf_op jit(solution)/shard_map/ppermute | solution.py:53
  162.4 6.1 %slice-start.1 = ((s8[6291456]{0:T(1024)(128)(4,1)}), s8[4194304]{0:T(1024)(128)(4,1)S(1)}, s32[]{:S(2)}) async-start(s8[6291456]{0:T(1024)(128)(4,1)} %bitcast.47), calls=%async_computation.7 | async-start | bytes 8388608
  165.8 2.7 copy-start
  297.5 11.9 %copy-start.1 = (bf16[1,2,8,48,4096]{4,3,2,1,0:T(8,128)(2,1)S(1)}, bf16[1,2,8,48,4096]{4,3,2,1,0:T(8,128)(2,1)}, u32[]{:S(2)}) copy-start(bf16[1,2,8,48,4096]{4,3,2,1,0:T(8,128)(2,1)} %copy-done) | copy-start | bytes 18874372
  297.5 11.9 %copy-start.5 = (f32[2,384,768]{2,1,0:T(8,128)S(1)}, f32[2,384,768]{2,1,0:T(8,128)}, u32[]{:S(2)}) copy-start(f32[2,384,768]{2,1,0:T(8,128)} %fusion.2) | copy-start | bytes 7077892
  483.8 6.3 %copy-start.4 = (f32[64,8]{0,1:T(8,128)S(1)}, f32[64,8]{0,1:T(8,128)}, u32[]{:S(2)}) copy-start(f32[64,8]{0,1:T(8,128)} %param.8) | copy-start | bytes 6148
  483.8 77.3 %all-to-all-start.1 = ((bf16[1,2,384,2048]{3,1,0,2:T(2,128)(2,1)}), bf16[1,2,384,2048]{3,1,0,2:T(2,128)(2,1)S(1)}, u32[]{:S(2)}, u32[]{:S(2)}) async-start(bf16[1,2,384,2048]{3,1,0,2:T(2,128)(2,1)} %copy.53), calls=%async_computation.2 | async-start | bytes 6291456 | tf_op jit(solution)/shard_map/all_to_all | solution.py:74
Sparse Core Ops, SparseCore 0:
  8.9 288.5 all-gather.2
  299.0 152.4 all-gather.4
  463.2 13.8 reduce-scatter.1
